TPU v7x, 32 devices: a whole 2x2x4 slice. The times are simulated.
32 devices in a mesh: owner: 4 (over y, core), rows: 8 (over z, x).
Axes of the slice: x: 2, y: 2, z: 4, core: 2. Of those that a mesh axis runs over, the one named last changes fastest.
Arguments:
- w_gate: float32 [128, 2048, 768], P('owner', 'rows'), may hold values from -0.125 to 0.125
- w_up: float32 [128, 2048, 768], P('owner', 'rows'), may hold values from -0.125 to 0.125
- router_weight: float32 [2048, 128], P('rows', 'owner'), may hold values from -0.125 to 0.125
- router_gain: float32 [2048], P('rows'), may hold values from 0.25 to 1.75
Outputs:
- serve_gate: bfloat16 [128, 768, 2048], P('owner', 'rows')
- serve_up: bfloat16 [128, 768, 2048], P('owner', 'rows')
- serve_router: bfloat16 [2048, 128], replicated
All inputs are finite; a program needn't handle non-finite values.
Results may differ from a plain program's by a relative error of at most 0.001.
Values may be sent and summed in bfloat16 or wider, within the bound.
A program may use at most 192 MiB of HBM per device.

v0:
```python
import jax
import jax.numpy as jnp
from jax import lax
from jax.sharding import PartitionSpec as P


def body(w_gate, w_up, router_weight, router_gain):
    narrow_gate, narrow_up = (w_gate.astype(jnp.bfloat16), w_up.astype(jnp.bfloat16))
    serve_gate, serve_up = (
        lax.all_to_all(narrow_gate, "rows", split_axis=2, concat_axis=1, tiled=True),
        lax.all_to_all(narrow_up, "rows", split_axis=2, concat_axis=1, tiled=True),
    )
    serve_gate = jnp.transpose(serve_gate, (0, 2, 1))
    serve_up = jnp.transpose(serve_up, (0, 2, 1))
    part_router = (router_weight * router_gain[:, None]).astype(jnp.bfloat16)
    row_router = lax.all_gather(part_router, "rows", axis=0, tiled=True)
    serve_router = lax.all_gather(row_router, "owner", axis=1, tiled=True)
    return (serve_gate, serve_up, serve_router)


def solution(mesh):
    placed = (P("owner", "rows", None), P("owner", "rows", None), P("rows", "owner"), P("rows"))
    return jax.shard_map(
        body,
        mesh=mesh,
        in_specs=placed,
        out_specs=(P("owner", "rows", None), P("owner", "rows", None), P()),
        check_vma=False,
    )
```

profile of v0, /device:TPU:0, one launch (start us, length us, event | category | flops | bytes accessed | tf_op | source)
XLA Modules:
  0.0 675.1 jit_solution(17104472041660287558)
XLA Ops:
  0.6 21.3 %copy.18 = bf16[32,256,768]{1,0,2:T(8,128)(2,1)} copy(f32[32,256,768]{2,1,0:T(8,128)} %param.4) | data formatting | bytes 37748736 | tf_op args[0]
  21.9 7.3 %all-to-all-start = ((bf16[32,256,768]{1,0,2:T(8,128)(2,1)}), bf16[32,256,768]{1,0,2:T(8,128)(2,1)}, u32[]{:S(2)}, u32[]{:S(2)}) async-start(bf16[32,256,768]{1,0,2:T(8,128)(2,1)} %copy.18), calls=%async_computation | async-start | bytes 25165824 | tf_op jit(solution)/shard_map/all_to_all | solution.py:10
  29.2 21.4 %copy.21 = bf16[32,256,768]{1,0,2:T(8,128)(2,1)} copy(f32[32,256,768]{2,1,0:T(8,128)} %param.5) | data formatting | bytes 37748736 | tf_op args[1]
  50.6 0.0 copy-start
  50.6 0.0 copy-start.1
  50.6 251.6 %all-to-all-done = bf16[32,256,768]{1,0,2:T(8,128)(2,1)} async-done(((bf16[32,256,768]{1,0,2:T(8,128)(2,1)}), bf16[32,256,768]{1,0,2:T(8,128)(2,1)}, u32[]{:S(2)}, u32[]{:S(2)}) %all-to-all-start) | async-done | bytes 12582944 | tf_op jit(solution)/shard_map/all_to_all | solution.py:10
  302.2 5.3 all-to-all-start.1
  307.6 0.0 copy-done
  307.6 0.0 copy-done.1
  307.6 292.2 %all_gather.6 = bf16[2048,32]{0,1:T(8,128)(2,1)S(1)} all-gather(bf16[256,32]{0,1:T(8,128)(2,1)S(1)} %multiply_convert_fusion), channel_id=1, replica_groups=mesh['owner'=4,'rows'=8] {'rows'}, dimensions={0}, use_global_device_ids=true | all-gather | bytes 147456 | tf_op jit(solution)/shard_map/all_gather | solution.py:16
  599.8 7.2 %all_gather.7 = bf16[2048,128]{0,1:T(8,128)(2,1)S(1)} all-gather(bf16[2048,32]{0,1:T(8,128)(2,1)S(1)} %all_gather.6), channel_id=1, replica_groups=mesh['owner'=4,'rows'=8] {'owner'}, dimensions={1}, use_global_device_ids=true | all-gather | bytes 655360 | tf_op jit(solution)/shard_map/all_gather | solution.py:17
  607.0 1.0 copy.24
  608.0 14.1 %copy.20 = bf16[32,8,256,96]{2,1,3,0:T(8,128)(2,1)} copy(bf16[32,8,256,96]{2,0,3,1:T(8,128)(2,1)} %bitcast.2) | data formatting | bytes 25165824 | tf_op jit(solution)/shard_map/all_to_all | solution.py:10
  622.1 19.5 %all_to_all.29 = bf16[32,2048,96]{1,2,0:T(8,128)(2,1)} reshape(bf16[32,8,256,96]{2,1,3,0:T(8,128)(2,1)} %copy.20) | data formatting | bytes 25165824 | tf_op jit(solution)/shard_map/all_to_all | solution.py:10
  641.6 0.0 all-to-all-done.1
  641.6 14.1 %copy.23 = bf16[32,8,256,96]{2,1,3,0:T(8,128)(2,1)} copy(bf16[32,8,256,96]{2,0,3,1:T(8,128)(2,1)} %bitcast.6) | data formatting | bytes 25165824 | tf_op jit(solution)/shard_map/all_to_all | solution.py:11
  655.7 19.5 %all_to_all.33 = bf16[32,2048,96]{1,2,0:T(8,128)(2,1)} reshape(bf16[32,8,256,96]{2,1,3,0:T(8,128)(2,1)} %copy.23) | data formatting | bytes 25165824 | tf_op jit(solution)/shard_map/all_to_all | solution.py:11
  (1 shorter events, 0.0 us)
Async XLA Ops:
  21.9 280.3 %all-to-all-start = ((bf16[32,256,768]{1,0,2:T(8,128)(2,1)}), bf16[32,256,768]{1,0,2:T(8,128)(2,1)}, u32[]{:S(2)}, u32[]{:S(2)}) async-start(bf16[32,256,768]{1,0,2:T(8,128)(2,1)} %copy.18), calls=%async_computation | async-start | bytes 25165824 | tf_op jit(solution)/shard_map/all_to_all | solution.py:10
  50.6 257.0 %copy-start = (f32[256,32]{0,1:T(8,128)S(1)}, f32[256,32]{0,1:T(8,128)}, u32[]{:S(2)}) copy-start(f32[256,32]{0,1:T(8,128)} %param.6) | copy-start | bytes 98308
  50.6 257.0 %copy-start.1 = (f32[256]{0:T(256)S(1)}, f32[256]{0:T(256)}, u32[]{:S(2)}) copy-start(f32[256]{0:T(256)} %param.7) | copy-start | bytes 3076
  302.2 339.3 %all-to-all-start.1 = ((bf16[32,256,768]{1,0,2:T(8,128)(2,1)}), bf16[32,256,768]{1,0,2:T(8,128)(2,1)}, u32[]{:S(2)}, u32[]{:S(2)}) async-start(bf16[32,256,768]{1,0,2:T(8,128)(2,1)} %copy.21), calls=%async_computation.1 | async-start | bytes 25165824 | tf_op jit(solution)/shard_map/all_to_all | solution.py:11
where the time goes:
time: 677 us; the launch traced here: 675 us
  blocking collectives  299 us (44%)
  waiting for transfers between devices  252 us (37%)
  local copies, waits for them, and re-layouts  111 us (16%)
  starting transfers between devices  12.6 us (2%)
    all_gather x1, blocking collectives, body(): row_router = lax.all_gather(part_router, 'rows', axis=0, tiled=True)  292 us
    all_to_all x1, waiting for transfers between devices, body(): lax.all_to_all(narrow_gate, 'rows', split_axis=2, concat_axis=1, tiled=True)  252 us
    unnamed x7, local copies, waits for them, and re-layouts  43.7 us
    all_to_all x2, local copies, waits for them, and re-layouts, body(): lax.all_to_all(narrow_up, 'rows', split_axis=2, concat_axis=1, tiled=True)  33.6 us
    all_to_all x2, local copies, waits for them, and re-layouts, body(): lax.all_to_all(narrow_gate, 'rows', split_axis=2, concat_axis=1, tiled=True)  33.5 us
  transfers between devices with their start and end apart: 2, of which 1 were waited for; matrix products, arithmetic and copies ran while one was open for 5% of the time, Pallas kernels for 0%

commit v1 on v0

--- a/solution.py
+++ b/solution.py
@@ -1,10 +1,179 @@
+import functools
+
 import jax
 import jax.numpy as jnp
 from jax import lax
+from jax.experimental import pallas as pl
+from jax.experimental.pallas import tpu as pltpu
 from jax.sharding import PartitionSpec as P
 
-
-def body(w_gate, w_up, router_weight, router_gain):
+MESH = pl.DeviceIdType.MESH
+SLOTS = 4
+
+
+def flipped(me, k):
+    out, bit = me, 1
+    while bit <= k:
+        if k & bit:
+            out = out + bit * (1 - 2 * ((me // bit) % 2))
+        bit *= 2
+    return out
+
+
+def exchange(rows, owners, gate_ref, up_ref, router_ref, sgate_ref, sup_ref, srouter_ref,
+             taken, turned, read_sem, send_sem, recv_sem, keep_sem, rsend, rrecv, osend, orecv, rkeep):
+    me, mine = lax.axis_index("rows"), lax.axis_index("owner")
+    experts, depth, width = gate_ref.shape
+    part = width // rows
+    share = router_ref.shape[0]
+    sources, results = (gate_ref, up_ref), (sgate_ref, sup_ref)
+    half = rows // 2
+    quarter = (me * 4) // rows
+    outer = (quarter == 0) | (quarter == 3)
+
+    barrier = pltpu.get_barrier_semaphore()
+    for k in range(1, rows):
+        pl.semaphore_signal(barrier, inc=1, device_id={"rows": flipped(me, k)}, device_id_type=MESH)
+    for k in range(1, owners):
+        pl.semaphore_signal(barrier, inc=1, device_id={"owner": lax.rem(mine + k, owners)}, device_id_type=MESH)
+
+    def reading(b, e, m):
+        return pltpu.make_async_copy(sources[m].at[e], taken.at[b], read_sem.at[b])
+
+    def place(d, size):
+        return pl.ds(pl.multiple_of(d * size, size), size)
+
+    def sending(m, k, which):
+        there = flipped(me, k)
+        return pltpu.make_async_remote_copy(
+            src_ref=turned.at[m, which, place(there, part), :],
+            dst_ref=results[m].at[which, :, place(me, depth)],
+            send_sem=send_sem.at[m, k],
+            recv_sem=recv_sem.at[m, k],
+            device_id={"rows": there},
+            device_id_type=MESH,
+        )
+
+    def router_rows(k):
+        return pltpu.make_async_remote_copy(
+            src_ref=router_ref,
+            dst_ref=srouter_ref.at[place(mine, share), place(me, depth)],
+            send_sem=rsend.at[k], recv_sem=rrecv.at[k],
+            device_id={"rows": flipped(me, k)}, device_id_type=MESH,
+        )
+
+    def router_owner(k):
+        return pltpu.make_async_remote_copy(
+            src_ref=srouter_ref.at[place(mine, share), :],
+            dst_ref=srouter_ref.at[place(mine, share), :],
+            send_sem=osend.at[k], recv_sem=orecv.at[k],
+            device_id={"owner": lax.rem(mine + k, owners)}, device_id_type=MESH,
+        )
+
+    router_keep = pltpu.make_async_copy(
+        router_ref, srouter_ref.at[place(mine, share), place(me, depth)], rkeep)
+
+    for b in range(SLOTS):
+        reading(b, b // 2, b % 2).start()
+    pl.semaphore_wait(barrier, rows - 1 + owners - 1)
+    router_keep.start()
+    for k in range(1, rows):
+        router_rows(k).start()
+
+    far = [k for k in range(rows - 1, half - 1, -1)]
+    near = [k for k in range(half - 1, 0, -1)]
+
+    def send_block(e, m):
+        @pl.when(jnp.logical_not(outer))
+        def _():
+            for k in far:
+                sending(m, k, pl.ds(e, 1)).start()
+        for k in near:
+            sending(m, k, pl.ds(e, 1)).start()
+
+    def turn(b, e, m):
+        reading(b, e, m).wait()
+        for j in range(width // 128):
+            block = taken[b, :, j * 128:(j + 1) * 128].astype(jnp.bfloat16)
+            turned[m, e, j * 128:(j + 1) * 128, :] = block.T
+
+    per = SLOTS // 2
+
+    def step(i, carry):
+        for q in range(per):
+            for m in range(2):
+                e, b = i * per + q, q * 2 + m
+                turn(b, e, m)
+
+                @pl.when(e + per < experts)
+                def _():
+                    reading(b, e + per, m).start()
+            for m in range(2):
+                send_block(i * per + q, m)
+        return carry
+
+    lax.fori_loop(0, experts // per, step, 0)
+
+    every = pl.ds(0, experts)
+
+    @pl.when(outer)
+    def _():
+        for m in range(2):
+            for k in far:
+                sending(m, k, every).start()
+
+    keeps = [pltpu.make_async_copy(
+        turned.at[m, :, place(me, part), :], results[m].at[:, :, place(me, depth)], keep_sem.at[m])
+        for m in range(2)]
+    for copy in keeps:
+        copy.start()
+    router_keep.wait()
+    for k in range(1, rows):
+        router_rows(k).wait()
+    for k in range(1, owners):
+        router_owner(k).start()
+    for k in range(1, owners):
+        router_owner(k).wait()
+    for copy in keeps:
+        copy.wait()
+    for m in range(2):
+        for k in range(1, rows):
+            sending(m, k, every).wait()
+
+
+def fused(rows, owners, w_gate, w_up, router_weight, router_gain):
+    experts, depth, width = w_gate.shape
+    share = router_weight.shape[1]
+    part_router = (router_weight * router_gain[:, None]).astype(jnp.bfloat16).T
+    out = jax.ShapeDtypeStruct((experts, width // rows, depth * rows), jnp.bfloat16)
+    sems = pltpu.SemaphoreType.DMA
+    sent = 2 * experts * depth * width * 2
+    serve_gate, serve_up, router = pl.pallas_call(
+        functools.partial(exchange, rows, owners),
+        out_shape=(out, out, jax.ShapeDtypeStruct((share * owners, depth * rows), jnp.bfloat16)),
+        in_specs=[pl.BlockSpec(memory_space=pl.ANY)] * 2 + [pl.BlockSpec(memory_space=pltpu.VMEM)],
+        out_specs=[pl.BlockSpec(memory_space=pl.ANY)] * 3,
+        scratch_shapes=[
+            pltpu.VMEM((SLOTS, depth, width), jnp.float32),
+            pltpu.VMEM((2, experts, width, depth), jnp.bfloat16),
+            sems((SLOTS,)),
+            sems((2, rows)),
+            sems((2, rows)),
+            sems((2,)),
+            sems((rows,)),
+            sems((rows,)),
+            sems((owners,)),
+            sems((owners,)),
+            sems,
+        ],
+        compiler_params=pltpu.CompilerParams(
+            collective_id=0, has_side_effects=True, vmem_limit_bytes=60 * 1024 * 1024),
+        cost_estimate=pl.CostEstimate(flops=0, bytes_accessed=4 * sent, transcendentals=0),
+    )(w_gate, w_up, part_router)
+    return serve_gate, serve_up, router.T
+
+
+def plain(w_gate, w_up, router_weight, router_gain):
     narrow_gate, narrow_up = (w_gate.astype(jnp.bfloat16), w_up.astype(jnp.bfloat16))
     serve_gate, serve_up = (
         lax.all_to_all(narrow_gate, "rows", split_axis=2, concat_axis=1, tiled=True),
@@ -19,6 +188,21 @@
 
 
 def solution(mesh):
+    rows, owners = mesh.shape["rows"], mesh.shape["owner"]
+
+    def body(w_gate, w_up, router_weight, router_gain):
+        experts, depth, width = w_gate.shape
+        share = router_weight.shape[1]
+        aligned = (
+            depth % 128 == 0 and width % 128 == 0 and width % (16 * rows) == 0
+            and share % 16 == 0 and experts % (SLOTS // 2) == 0
+            and rows >= 4 and rows & (rows - 1) == 0
+            and 2 * experts * depth * width * 2 + SLOTS * depth * width * 4 <= 56 * 1024 * 1024
+        )
+        if aligned:
+            return fused(rows, owners, w_gate, w_up, router_weight, router_gain)
+        return plain(w_gate, w_up, router_weight, router_gain)
+
     placed = (P("owner", "rows", None), P("owner", "rows", None), P("rows", "owner"), P("rows"))
     return jax.shard_map(
         body,

time: 677 us -> 573 us (0.85)
  Pallas kernels: 0 us -> 550 us
  blocking collectives: 299 us -> 0 us
  waiting for transfers between devices: 252 us -> 0 us
  local copies, waits for them, and re-layouts: 111 us -> 19.7 us
  starting transfers between devices: 12.6 us -> 0 us
    pallas_call x0 -> x1, Pallas kernels: none -> 550 us  [fused(): pl.pallas_call(functools.partial(exchange, rows, owners), out_shape=(out,...]
    all_gather x2 -> x0, blocking collectives: 299 us -> none  [the longest x1 292 us: body(): row_router = lax.all_gather(part_router, 'rows', axis=0, tiled=True)]
    all_to_all x2 -> x0, waiting for transfers between devices: 252 us -> none  [the longest x1 252 us: body(): lax.all_to_all(narrow_gate, 'rows', split_axis=2, concat_axis=1, tiled=True)]
    all_to_all x4 -> x0, local copies, waits for them, and re-layouts: 67.1 us -> none  [the longest x2 33.6 us: body(): lax.all_to_all(narrow_up, 'rows', split_axis=2, concat_axis=1, tiled=True)]
    unnamed x7 -> x5, local copies, waits for them, and re-layouts: 43.7 us -> 19.7 us
    all_to_all x2 -> x0, starting transfers between devices: 12.6 us -> none  [the longest x1 7.28 us: body(): lax.all_to_all(narrow_gate, 'rows', split_axis=2, concat_axis=1, tiled=True)]
  transfers between devices with their start and end apart: 2 -> 0, of which waited for: 1 -> 0; matrix products, arithmetic and copies ran while one was open for 5% -> 0% of each run, Pallas kernels for 0% -> 0%
where the time goes in v1:
time: 573 us; the launch traced here: 572 us
  Pallas kernels  550 us (96%)
  local copies, waits for them, and re-layouts  19.7 us (3%)
    pallas_call x1, Pallas kernels, fused(): pl.pallas_call(functools.partial(exchange, rows, owners), out_shape=(out,...  550 us
    unnamed x5, local copies, waits for them, and re-layouts  19.7 us

profile of v1, /device:TPU:0, one launch (start us, length us, event | category | flops | bytes accessed | tf_op | source)
XLA Modules:
  0.0 572.2 jit_solution(16787071713636370546)
XLA Ops:
  0.6 1.4 fusion.router_ref
  2.0 550.5 %shard_map.67 = (bf16[32,96,2048]{2,1,0:T(8,128)(2,1)}, bf16[32,96,2048]{2,1,0:T(8,128)(2,1)}, bf16[128,2048]{1,0:T(8,128)(2,1)}) custom-call(f32[32,256,768]{2,1,0:T(8,128)} %gate_ref.1, f32[32,256,768]{2,1,0:T(8,128)} %up_ref.1, bf16[32,256]{1,0:T(8,128)(2,1)} %fusion.router_ref), custom_call_target="tpu_custom_call" | custom-call | bytes 100663296 | tf_op jit(solution)/shard_map/pallas_call | solution.py:151
  552.5 2.0 copy.7
  554.5 0.0 copy-start
  554.5 11.4 %copy.10 = bf16[32,96,2048]{2,1,0:T(8,128)(2,1)} copy(bf16[32,96,2048]{2,1,0:T(8,128)(2,1)} %get-tuple-element.15) | data formatting | bytes 25165824
  565.9 1.5 copy-done
  567.4 4.8 copy.11
Async XLA Ops:
  554.5 12.9 %copy-start = (bf16[32,96,2048]{2,1,0:T(8,128)(2,1)S(1)}, bf16[32,96,2048]{2,1,0:T(8,128)(2,1)}, u32[]{:S(2)}) copy-start(bf16[32,96,2048]{2,1,0:T(8,128)(2,1)} %get-tuple-element.16) | copy-start | bytes 37748740

commit v2 on v1

--- a/solution.py
+++ b/solution.py
@@ -20,12 +20,12 @@
     return out
 
 
-def exchange(rows, owners, gate_ref, up_ref, router_ref, sgate_ref, sup_ref, srouter_ref,
-             taken, turned, read_sem, send_sem, recv_sem, keep_sem, rsend, rrecv, osend, orecv, rkeep):
+def exchange(rows, owners, gate_ref, up_ref, weight_ref, gain_ref, sgate_ref, sup_ref, srouter_ref,
+             router_ref, taken, turned, read_sem, send_sem, recv_sem, keep_sem, rsend, rrecv, osend, orecv, rkeep):
     me, mine = lax.axis_index("rows"), lax.axis_index("owner")
     experts, depth, width = gate_ref.shape
     part = width // rows
-    share = router_ref.shape[0]
+    share = weight_ref.shape[0]
     sources, results = (gate_ref, up_ref), (sgate_ref, sup_ref)
     half = rows // 2
     quarter = (me * 4) // rows
@@ -75,11 +75,8 @@
 
     for b in range(SLOTS):
         reading(b, b // 2, b % 2).start()
+    router_ref[...] = (weight_ref[...] * gain_ref[...]).astype(jnp.bfloat16)
     pl.semaphore_wait(barrier, rows - 1 + owners - 1)
-    router_keep.start()
-    for k in range(1, rows):
-        router_rows(k).start()
-
     far = [k for k in range(rows - 1, half - 1, -1)]
     near = [k for k in range(half - 1, 0, -1)]
 
@@ -97,22 +94,29 @@
             block = taken[b, :, j * 128:(j + 1) * 128].astype(jnp.bfloat16)
             turned[m, e, j * 128:(j + 1) * 128, :] = block.T
 
+    def advance(b, e, m):
+        turn(b, e, m)
+
+        @pl.when(e + per < experts)
+        def _():
+            reading(b, e + per, m).start()
+
     per = SLOTS // 2
-
-    def step(i, carry):
-        for q in range(per):
-            for m in range(2):
-                e, b = i * per + q, q * 2 + m
-                turn(b, e, m)
-
-                @pl.when(e + per < experts)
-                def _():
-                    reading(b, e + per, m).start()
-            for m in range(2):
-                send_block(i * per + q, m)
+    advance(0, 0, 0)
+    advance(1, 0, 1)
+    send_block(0, 0)
+    router_keep.start()
+    for k in range(1, rows):
+        router_rows(k).start()
+
+    def step(e, carry):
+        for m in range(2):
+            advance(2 * lax.rem(e, per) + m, e, m)
+            send_block(e - 1 + m, 1 - m)
         return carry
 
-    lax.fori_loop(0, experts // per, step, 0)
+    lax.fori_loop(1, experts, step, 0)
+    send_block(experts - 1, 1)
 
     every = pl.ds(0, experts)
 
@@ -144,16 +148,16 @@
 def fused(rows, owners, w_gate, w_up, router_weight, router_gain):
     experts, depth, width = w_gate.shape
     share = router_weight.shape[1]
-    part_router = (router_weight * router_gain[:, None]).astype(jnp.bfloat16).T
     out = jax.ShapeDtypeStruct((experts, width // rows, depth * rows), jnp.bfloat16)
     sems = pltpu.SemaphoreType.DMA
     sent = 2 * experts * depth * width * 2
     serve_gate, serve_up, router = pl.pallas_call(
         functools.partial(exchange, rows, owners),
         out_shape=(out, out, jax.ShapeDtypeStruct((share * owners, depth * rows), jnp.bfloat16)),
-        in_specs=[pl.BlockSpec(memory_space=pl.ANY)] * 2 + [pl.BlockSpec(memory_space=pltpu.VMEM)],
+        in_specs=[pl.BlockSpec(memory_space=pl.ANY)] * 2 + [pl.BlockSpec(memory_space=pltpu.VMEM)] * 2,
         out_specs=[pl.BlockSpec(memory_space=pl.ANY)] * 3,
         scratch_shapes=[
+            pltpu.VMEM((share, depth), jnp.bfloat16),
             pltpu.VMEM((SLOTS, depth, width), jnp.float32),
             pltpu.VMEM((2, experts, width, depth), jnp.bfloat16),
             sems((SLOTS,)),
@@ -169,7 +173,7 @@
         compiler_params=pltpu.CompilerParams(
             collective_id=0, has_side_effects=True, vmem_limit_bytes=60 * 1024 * 1024),
         cost_estimate=pl.CostEstimate(flops=0, bytes_accessed=4 * sent, transcendentals=0),
-    )(w_gate, w_up, part_router)
+    )(w_gate, w_up, router_weight.T, router_gain[None, :])
     return serve_gate, serve_up, router.T
 
 

time: 573 us -> 572 us (level)
  no operation moved by 1% of the time
where the time goes in v2:
time: 572 us; the launch traced here: 571 us
  Pallas kernels  551 us (96%)
  local copies, waits for them, and re-layouts  19.7 us (3%)
    pallas_call x1, Pallas kernels, fused(): pl.pallas_call(functools.partial(exchange, rows, owners), out_shape=(out,...  551 us
    unnamed x5, local copies, waits for them, and re-layouts  19.7 us

profile of v2, /device:TPU:0, one launch (start us, length us, event | category | flops | bytes accessed | tf_op | source)
XLA Modules:
  0.0 571.2 jit_solution(2760315717133870444)
XLA Ops:
  0.6 550.9 %shard_map.67 = (bf16[32,96,2048]{2,1,0:T(8,128)(2,1)}, bf16[32,96,2048]{2,1,0:T(8,128)(2,1)}, bf16[128,2048]{1,0:T(8,128)(2,1)}) custom-call(f32[32,256,768]{2,1,0:T(8,128)} %gate_ref.1, f32[32,256,768]{2,1,0:T(8,128)} %up_ref.1, f32[32,256]{1,0:T(8,128)} %bitcast.4, f32[1,256]{1,0:T(1,128)} %bitcast.5), custom_call_target="tpu_custom_call" | custom-call | bytes 100663296 | tf_op jit(solution)/shard_map/pallas_call | solution.py:154
  551.5 2.0 copy.7
  553.5 0.0 copy-start
  553.5 11.4 %copy.10 = bf16[32,96,2048]{2,1,0:T(8,128)(2,1)} copy(bf16[32,96,2048]{2,1,0:T(8,128)(2,1)} %get-tuple-element.15) | data formatting | bytes 25165824
  564.9 1.5 copy-done
  566.4 4.8 copy.11
Async XLA Ops:
  553.5 12.9 %copy-start = (bf16[32,96,2048]{2,1,0:T(8,128)(2,1)S(1)}, bf16[32,96,2048]{2,1,0:T(8,128)(2,1)}, u32[]{:S(2)}) copy-start(bf16[32,96,2048]{2,1,0:T(8,128)(2,1)} %get-tuple-element.16) | copy-start | bytes 37748740
